TPU v7x, 32 devices: a whole 2x2x4 slice. The times are simulated.
32 devices in a mesh: grp: 4 (over y, x), dev: 8 (over z, core).
Axes of the slice: x: 2, y: 2, z: 4, core: 2. Of those that a mesh axis runs over, the one named last changes fastest.
Arguments:
- embeddings: bfloat16 [262144, 256], P(('grp', 'dev'))
- prior_dist: float32 [262144], P(('grp', 'dev')), may hold values from 1 to 3
- seed_ids: int32 [6, 512], replicated, may hold values from 0 to 262143, as said below
Outputs:
- min_dist: float32 [262144], P(('grp', 'dev'))
- group_means: float32 [6, 4], P(None, 'grp')
Inputs may be any that keep to these rules, and one draw needn't show every extreme that they name: `seed_ids`: round r's ids all lie in the rows of group r mod 4, that is from (r mod 4) * 65536 to (r mod 4 + 1) * 65536 - 1; ids may repeat.
All inputs are finite; a program needn't handle non-finite values.
Results may differ from a plain program's by a relative error of at most 0.0003.
Values may be sent and summed in bfloat16 or wider, within the bound.
No kernel may reach another device: no remote copies, remote signals or barrier semaphores. Data moves between devices by JAX's collectives and lax.ppermute only.
A program may use at most 64 MiB of HBM per device.

v0:
```python
import jax
import jax.numpy as jnp
from jax import lax
from jax.sharding import PartitionSpec as P


def block_gaps(block, block_norms, centers, seed_norms, feature_dim):
    products = jnp.dot(block, centers.T, preferred_element_type=jnp.float32)
    return jnp.maximum(block_norms[:, None] + seed_norms[None, :] - 2.0 * products, 0.0) / float(
        feature_dim
    )


def body(embeddings, prior_dist, seed_ids):
    row_count, feature_dim = embeddings.shape
    round_count, seed_count = seed_ids.shape
    dev_count = lax.axis_size("dev")
    row_start = (lax.axis_index("grp") * dev_count + lax.axis_index("dev")) * row_count
    offsets = seed_ids - row_start
    inside = (offsets >= 0) & (offsets < row_count)
    picked = jnp.take(embeddings, jnp.clip(offsets, 0, row_count - 1), axis=0)
    picked = jnp.where(inside[:, :, None], picked.astype(jnp.float32), 0.0)
    owned = lax.psum(picked.astype(jnp.bfloat16), "dev")
    summed = lax.psum(owned, "grp")
    centers = [summed[round_index] for round_index in range(round_count)]
    seed_norms = [jnp.sum(jnp.square(center.astype(jnp.float32)), axis=1) for center in centers]
    row_norms = jnp.sum(jnp.square(embeddings.astype(jnp.float32)), axis=1)
    block_rows = min(2048, row_count)
    block_count = row_count // block_rows
    blocks = embeddings.reshape(block_count, block_rows, feature_dim)
    norm_blocks = row_norms.reshape(block_count, block_rows)
    per_round = []
    for round_index in range(round_count):
        center = centers[round_index]
        center_norms = seed_norms[round_index]

        def one_round(pair, center=center, center_norms=center_norms):
            return jnp.min(block_gaps(pair[0], pair[1], center, center_norms, feature_dim), axis=1)

        per_round.append(lax.map(one_round, (blocks, norm_blocks)).reshape(row_count))
    group_total = float(row_count * dev_count)
    current = prior_dist
    collected = []
    for round_index in range(round_count):
        current = jnp.minimum(current, per_round[round_index])
        collected.append(lax.psum(jnp.sum(current), "dev") / group_total)
    means = jnp.stack(collected)
    return (current, means.reshape(round_count, 1))


def solution(mesh):
    placed = (P(("grp", "dev"), None), P(("grp", "dev")), P())
    return jax.shard_map(
        body,
        mesh=mesh,
        in_specs=placed,
        out_specs=(P(("grp", "dev")), P(None, "grp")),
        check_vma=False,
    )
```

profile of v0, /device:TPU:0, one launch (start us, length us, event | category | flops | bytes accessed | tf_op | source)
XLA Modules:
  0.0 242.5 jit_solution(16635363489336066395)
XLA Ops:
  7.2 0.7 compare_and_fusion
  8.0 12.5 %gather_fusion = bf16[3072,256]{1,0:T(8,128)(2,1)S(1)} fusion(bf16[8192,256]{1,0:T(8,128)(2,1)} %param.15, s32[3072]{0:T(1024)S(1)} %broadcast_clamp_fusion), kind=kCustom, calls=%fused_computation | custom fusion | bytes 3158016 | tf_op jit(solution)/shard_map/jit(_take)/gather | solution.py:21
  20.5 2.4 select_convert_fusion
  23.0 64.7 %all-reduce.4.cloned.1.call-done = bf16[6,512,256]{2,1,0:T(8,128)(2,1)} async-done(((bf16[6,512,256]{2,1,0:T(8,128)(2,1)}), bf16[6,512,256]{2,1,0:T(8,128)(2,1)}) %all-reduce.4.cloned.1.call-update) | async-done | bytes 1572880 | tf_op jit(solution)/shard_map/psum | solution.py:23
  87.7 3.3 %multiply_reduce_fusion.6 = f32[8192]{0:T(1024)S(1)} fusion(bf16[8192,256]{1,0:T(8,128)(2,1)} %param.15), kind=kLoop, calls=%fused_computation.31 | loop fusion | flops 6283264 | bytes 4227072 | tf_op jit(solution)/shard_map/reduce_sum | solution.py:27
  91.0 59.7 %all-reduce.6.cloned.1.call-done = bf16[6,512,256]{2,1,0:T(8,128)(2,1)} async-done(((bf16[6,512,256]{2,1,0:T(8,128)(2,1)}), bf16[6,512,256]{2,1,0:T(8,128)(2,1)}) %all-reduce.6.cloned.1.call-update) | async-done | bytes 1572880 | tf_op jit(solution)/shard_map/psum | solution.py:24
  150.7 1.6 slice_bitcast_fusion.5
  152.3 0.3 copy-done
  152.6 0.5 multiply_reduce_fusion.8
  153.1 9.9 %while.62 = (s32[]{:T(128)}, f32[4,2048]{1,0:T(4,128)S(1)}, f32[4,2048]{1,0:T(4,128)S(1)}, f32[512]{0:T(512)S(1)}, bf16[4,2048,256]{2,1,0:T(8,128)(2,1)}, /*inde...) while((s32[]{:T(128)}, f32[4,2048]{1,0:T(4,128)S(1)}, f32[4,2048]{1,0:T(4,128)S(1)}, f32[512]{0:T(512)S(1)}, ...), condition=%wide.region_14.15_spmd, body=%wide.region_12.14_spmd.sunk | while | flops 543160320 | bytes 1362525 | solution.py:40
  153.1 2.3 multiply_reduce_fusion.21
  155.4 0.1 dynamic_update_slice.27
  155.6 2.3 multiply_reduce_fusion.21
  157.9 0.1 dynamic_update_slice.27
  158.1 2.3 multiply_reduce_fusion.21
  160.4 0.1 dynamic_update_slice.27
  160.5 2.3 multiply_reduce_fusion.21
  162.8 0.1 dynamic_update_slice.27
  163.0 9.9 %while.64 = (s32[]{:T(128)}, f32[4,2048]{1,0:T(4,128)S(1)}, f32[4,2048]{1,0:T(4,128)S(1)}, f32[512]{0:T(512)S(1)}, bf16[4,2048,256]{2,1,0:T(8,128)(2,1)}, /*inde...) while((s32[]{:T(128)}, f32[4,2048]{1,0:T(4,128)S(1)}, f32[4,2048]{1,0:T(4,128)S(1)}, f32[512]{0:T(512)S(1)}, ...), condition=%wide.region_22.23_spmd, body=%wide.region_20.22_spmd.sunk | while | flops 543160320 | bytes 1362525 | solution.py:40
  163.0 2.3 multiply_reduce_fusion.23
  165.3 0.1 dynamic_update_slice.29
  165.5 2.3 multiply_reduce_fusion.23
  168.0 2.3 multiply_reduce_fusion.23
  170.4 2.3 multiply_reduce_fusion.23
  172.9 9.9 %while.60 = (s32[]{:T(128)}, f32[4,2048]{1,0:T(4,128)S(1)}, f32[4,2048]{1,0:T(4,128)S(1)}, f32[512]{0:T(512)S(1)}, bf16[4,2048,256]{2,1,0:T(8,128)(2,1)}, /*inde...) while((s32[]{:T(128)}, f32[4,2048]{1,0:T(4,128)S(1)}, f32[4,2048]{1,0:T(4,128)S(1)}, f32[512]{0:T(512)S(1)}, ...), condition=%wide.region_6.7_spmd, body=%wide.region_4.6_spmd.sunk | while | flops 543160320 | bytes 1362525 | solution.py:40
  172.9 2.3 multiply_reduce_fusion.19
  175.4 2.3 multiply_reduce_fusion.19
  177.9 2.3 multiply_reduce_fusion.19
  180.3 2.3 multiply_reduce_fusion.19
  182.8 9.9 %while.61 = (s32[]{:T(128)}, f32[4,2048]{1,0:T(4,128)S(1)}, f32[4,2048]{1,0:T(4,128)S(1)}, f32[512]{0:T(512)S(1)}, bf16[4,2048,256]{2,1,0:T(8,128)(2,1)}, /*inde...) while((s32[]{:T(128)}, f32[4,2048]{1,0:T(4,128)S(1)}, f32[4,2048]{1,0:T(4,128)S(1)}, f32[512]{0:T(512)S(1)}, ...), condition=%wide.region_10.11_spmd, body=%wide.region_8.10_spmd.sunk | while | flops 543160320 | bytes 1362525 | solution.py:40
  182.8 2.3 multiply_reduce_fusion.20
  185.3 2.3 multiply_reduce_fusion.20
  187.7 2.3 multiply_reduce_fusion.20
  190.2 2.3 multiply_reduce_fusion.20
  192.7 9.8 %while.63 = (s32[]{:T(128)}, f32[4,2048]{1,0:T(4,128)S(1)}, f32[4,2048]{1,0:T(4,128)S(1)}, f32[512]{0:T(512)S(1)}, bf16[4,2048,256]{2,1,0:T(8,128)(2,1)}, /*inde...) while((s32[]{:T(128)}, f32[4,2048]{1,0:T(4,128)S(1)}, f32[4,2048]{1,0:T(4,128)S(1)}, f32[512]{0:T(512)S(1)}, ...), condition=%wide.region_18.19_spmd, body=%wide.region_16.18_spmd.sunk | while | flops 543160320 | bytes 1362525 | solution.py:40
  192.7 2.3 multiply_reduce_fusion.22
  195.2 2.3 multiply_reduce_fusion.22
  197.6 2.3 multiply_reduce_fusion.22
  200.1 2.3 multiply_reduce_fusion.22
  202.6 9.8 %while.65 = (s32[]{:T(128)}, f32[4,2048]{1,0:T(4,128)S(1)}, f32[4,2048]{1,0:T(4,128)S(1)}, f32[512]{0:T(512)S(1)}, bf16[4,2048,256]{2,1,0:T(8,128)(2,1)}, /*inde...) while((s32[]{:T(128)}, f32[4,2048]{1,0:T(4,128)S(1)}, f32[4,2048]{1,0:T(4,128)S(1)}, f32[512]{0:T(512)S(1)}, ...), condition=%wide.region_26.27_spmd, body=%wide.region_24.26_spmd.sunk | while | flops 543160320 | bytes 1362525 | solution.py:40
  202.6 2.3 multiply_reduce_fusion.24
  205.1 2.3 multiply_reduce_fusion.24
  207.5 2.3 multiply_reduce_fusion.24
  210.0 2.3 multiply_reduce_fusion.24
  212.4 1.2 fusion.18
  213.7 0.7 minimum_reduce_fusion
  214.4 16.9 %all-reduce = (f32[]{:T(128)}, f32[]{:T(128)}, f32[]{:T(128)}, f32[]{:T(128)}, f32[]{:T(128)}, /*index=5*/f32[]{:T(128)}) all-reduce(f32[]{:T(128)} %get-tuple-element.300, f32[]{:T(128)} %get-tuple-element.302, f32[]{:T(128)} %get-tuple-element.303, f32[]{:T(128)} %get-tuple-element.207, ...), channel_id=1, replica_groups=mesh['grp'=4,'dev'=8] {'dev'}, use_global_device_ids=true, to_apply=%region_28.29 | all-reduce | flops 6 | bytes 48 | tf_op jit(solution)/shard_map/psum | solution.py:46
  235.1 0.6 stack.27
  (65 shorter events, 2.9 us)
Async XLA Ops:
  7.2 80.5 %all-reduce.4.cloned.1.call-start = ((), (), s32[]{:S(2)}) async-start(), calls=%async_computation | async-start | bytes 3145728 | tf_op jit(solution)/shard_map/psum | solution.py:23
  22.9 127.8 %all-reduce.6.cloned.1.call-start = ((), (), s32[]{:S(2)}) async-start(), calls=%async_computation.1 | async-start | bytes 3145728 | tf_op jit(solution)/shard_map/psum | solution.py:24
  150.7 1.9 copy-start
  202.5 9.9 %copy-start.1 = (f32[8192]{0:T(1024)S(1)}, f32[8192]{0:T(1024)}, u32[]{:S(2)}) copy-start(f32[8192]{0:T(1024)} %param.16) | copy-start | bytes 98308
Sparse Core Ops, SparseCore 0:
  23.1 64.5 all-reduce.3
  90.7 59.9 all-reduce.5
where the time goes:
time: 244 us; the launch traced here: 243 us
  waiting for transfers between devices  124 us (51%)
  matrix products  54.8 us (22%)
  local copies, waits for them, and re-layouts  18.5 us (8%)
  between operations  18 us (7%)
  blocking collectives  16.9 us (7%)
  other arithmetic  8.89 us (4%)
    psum x1, waiting for transfers between devices, body(): owned = lax.psum(picked.astype(jnp.bfloat16), 'dev')  64.7 us
    psum x1, waiting for transfers between devices, body(): summed = lax.psum(owned, 'grp')  59.7 us
    dot_general x24, matrix products, block_gaps(): products = jnp.dot(block, centers.T, preferred_element_type=jnp.float32)  54.8 us
    psum x1, blocking collectives, body(): collected.append(lax.psum(jnp.sum(current), 'dev') / group_total)  16.9 us
    gather x1, local copies, waits for them, and re-layouts, body(): picked = jnp.take(embeddings, jnp.clip(offsets, 0, row_count - 1), axis=0)  12.5 us
  transfers between devices with their start and end apart: 2, of which 2 were waited for; matrix products, arithmetic and copies ran while one was open for 1% of the time, Pallas kernels for 0%

commit v1 on v0

--- a/solution.py
+++ b/solution.py
@@ -20,7 +20,7 @@
     inside = (offsets >= 0) & (offsets < row_count)
     picked = jnp.take(embeddings, jnp.clip(offsets, 0, row_count - 1), axis=0)
     picked = jnp.where(inside[:, :, None], picked.astype(jnp.float32), 0.0)
-    owned = lax.psum(picked.astype(jnp.bfloat16), "dev")
+    owned = jnp.sum(lax.all_gather(picked.astype(jnp.bfloat16), "dev"), axis=0)
     summed = lax.psum(owned, "grp")
     centers = [summed[round_index] for round_index in range(round_count)]
     seed_norms = [jnp.sum(jnp.square(center.astype(jnp.float32)), axis=1) for center in centers]

time: 244 us -> 303 us (1.24)
  waiting for transfers between devices: 124 us -> 175 us
  other arithmetic: 8.89 us -> 17 us
    all_gather x0 -> x1, waiting for transfers between devices: none -> 120 us  [body(): owned = jnp.sum(lax.all_gather(picked.astype(jnp.bfloat16), 'dev'), axis=0)]
    psum x1 -> x0, waiting for transfers between devices: 64.7 us -> none  [body(): owned = lax.psum(picked.astype(jnp.bfloat16), 'dev')]
    reduce_sum x0 -> x1, other arithmetic: none -> 8.15 us  [body(): owned = jnp.sum(lax.all_gather(picked.astype(jnp.bfloat16), 'dev'), axis=0)]
    psum x1, waiting for transfers between devices: 59.7 us -> 55.7 us  [body(): summed = lax.psum(owned, 'grp')]
where the time goes in v1:
time: 303 us; the launch traced here: 302 us
  waiting for transfers between devices  175 us (58%)
  matrix products  54.8 us (18%)
  local copies, waits for them, and re-layouts  18.5 us (6%)
  between operations  18 us (6%)
  other arithmetic  17 us (6%)
  blocking collectives  16.9 us (6%)
    all_gather x1, waiting for transfers between devices, body(): owned = jnp.sum(lax.all_gather(picked.astype(jnp.bfloat16), 'dev'), axis=0)  120 us
    psum x1, waiting for transfers between devices, body(): summed = lax.psum(owned, 'grp')  55.7 us
    dot_general x24, matrix products, block_gaps(): products = jnp.dot(block, centers.T, preferred_element_type=jnp.float32)  54.8 us
    psum x1, blocking collectives, body(): collected.append(lax.psum(jnp.sum(current), 'dev') / group_total)  16.9 us
    gather x1, local copies, waits for them, and re-layouts, body(): picked = jnp.take(embeddings, jnp.clip(offsets, 0, row_count - 1), axis=0)  12.5 us
    reduce_sum x1, other arithmetic, body(): owned = jnp.sum(lax.all_gather(picked.astype(jnp.bfloat16), 'dev'), axis=0)  8.15 us
  transfers between devices with their start and end apart: 2, of which 2 were waited for; matrix products, arithmetic and copies ran while one was open for 1% of the time, Pallas kernels for 0%

profile of v1, /device:TPU:0, one launch (start us, length us, event | category | flops | bytes accessed | tf_op | source)
XLA Modules:
  0.0 301.5 jit_solution(17466541672110018886)
XLA Ops:
  7.2 0.7 compare_and_fusion
  8.0 12.5 %gather_fusion = bf16[3072,256]{1,0:T(8,128)(2,1)S(1)} fusion(bf16[8192,256]{1,0:T(8,128)(2,1)} %param.15, s32[3072]{0:T(1024)S(1)} %broadcast_clamp_fusion), kind=kCustom, calls=%fused_computation | custom fusion | bytes 3158016 | tf_op jit(solution)/shard_map/jit(_take)/gather | solution.py:21
  20.5 2.4 select_convert_fusion
  23.0 119.5 %all-gather.2.cloned.1.call-done = bf16[8,6,512,256]{3,2,1,0:T(8,128)(2,1)} async-done(((bf16[1,6,512,256]{3,2,1,0:T(8,128)(2,1)}), bf16[8,6,512,256]{3,2,1,0:T(8,128)(2,1)}) %all-gather.2.cloned.1.call-update) | async-done | bytes 12582928 | tf_op jit(solution)/shard_map/all_gather | solution.py:23
  142.5 8.1 %reduce_sum.130 = bf16[6,512,256]{2,1,0:T(8,128)(2,1)} reduce(bf16[8,6,512,256]{3,2,1,0:T(8,128)(2,1)} %all-gather.2.cloned.1.call-done, bf16[]{:T(256)} %constant.147.clone.1), dimensions={0}, to_apply=%region_1.2 | reduce | flops 5505024 | bytes 14155778 | tf_op jit(solution)/shard_map/reduce_sum | solution.py:23
  150.7 3.3 %multiply_reduce_fusion.6 = f32[8192]{0:T(1024)S(1)} fusion(bf16[8192,256]{1,0:T(8,128)(2,1)} %param.15), kind=kLoop, calls=%fused_computation.31 | loop fusion | flops 6283264 | bytes 4227072 | tf_op jit(solution)/shard_map/reduce_sum | solution.py:27
  154.0 55.7 %all-reduce.3.cloned.1.call-done = bf16[6,512,256]{2,1,0:T(8,128)(2,1)} async-done(((bf16[6,512,256]{2,1,0:T(8,128)(2,1)}), bf16[6,512,256]{2,1,0:T(8,128)(2,1)}) %all-reduce.3.cloned.1.call-update) | async-done | bytes 1572880 | tf_op jit(solution)/shard_map/psum | solution.py:24
  209.8 1.6 slice_bitcast_fusion.5
  211.3 0.3 copy-done
  211.6 0.5 multiply_reduce_fusion.8
  212.1 9.9 %while.62 = (s32[]{:T(128)}, f32[4,2048]{1,0:T(4,128)S(1)}, f32[4,2048]{1,0:T(4,128)S(1)}, f32[512]{0:T(512)S(1)}, bf16[4,2048,256]{2,1,0:T(8,128)(2,1)}, /*inde...) while((s32[]{:T(128)}, f32[4,2048]{1,0:T(4,128)S(1)}, f32[4,2048]{1,0:T(4,128)S(1)}, f32[512]{0:T(512)S(1)}, ...), condition=%wide.region_14.15_spmd, body=%wide.region_12.14_spmd.sunk | while | flops 543160320 | bytes 1362525 | solution.py:40
  212.2 2.3 multiply_reduce_fusion.21
  214.5 0.1 dynamic_update_slice.27
  214.6 2.3 multiply_reduce_fusion.21
  216.9 0.1 dynamic_update_slice.27
  217.1 2.3 multiply_reduce_fusion.21
  219.4 0.1 dynamic_update_slice.27
  219.6 2.3 multiply_reduce_fusion.21
  221.9 0.1 dynamic_update_slice.27
  222.1 9.9 %while.64 = (s32[]{:T(128)}, f32[4,2048]{1,0:T(4,128)S(1)}, f32[4,2048]{1,0:T(4,128)S(1)}, f32[512]{0:T(512)S(1)}, bf16[4,2048,256]{2,1,0:T(8,128)(2,1)}, /*inde...) while((s32[]{:T(128)}, f32[4,2048]{1,0:T(4,128)S(1)}, f32[4,2048]{1,0:T(4,128)S(1)}, f32[512]{0:T(512)S(1)}, ...), condition=%wide.region_22.23_spmd, body=%wide.region_20.22_spmd.sunk | while | flops 543160320 | bytes 1362525 | solution.py:40
  222.1 2.3 multiply_reduce_fusion.23
  224.5 2.3 multiply_reduce_fusion.23
  227.0 2.3 multiply_reduce_fusion.23
  229.5 2.3 multiply_reduce_fusion.23
  231.9 9.9 %while.60 = (s32[]{:T(128)}, f32[4,2048]{1,0:T(4,128)S(1)}, f32[4,2048]{1,0:T(4,128)S(1)}, f32[512]{0:T(512)S(1)}, bf16[4,2048,256]{2,1,0:T(8,128)(2,1)}, /*inde...) while((s32[]{:T(128)}, f32[4,2048]{1,0:T(4,128)S(1)}, f32[4,2048]{1,0:T(4,128)S(1)}, f32[512]{0:T(512)S(1)}, ...), condition=%wide.region_6.7_spmd, body=%wide.region_4.6_spmd.sunk | while | flops 543160320 | bytes 1362525 | solution.py:40
  232.0 2.3 multiply_reduce_fusion.19
  234.4 2.3 multiply_reduce_fusion.19
  236.9 2.3 multiply_reduce_fusion.19
  239.4 2.3 multiply_reduce_fusion.19
  241.8 9.9 %while.61 = (s32[]{:T(128)}, f32[4,2048]{1,0:T(4,128)S(1)}, f32[4,2048]{1,0:T(4,128)S(1)}, f32[512]{0:T(512)S(1)}, bf16[4,2048,256]{2,1,0:T(8,128)(2,1)}, /*inde...) while((s32[]{:T(128)}, f32[4,2048]{1,0:T(4,128)S(1)}, f32[4,2048]{1,0:T(4,128)S(1)}, f32[512]{0:T(512)S(1)}, ...), condition=%wide.region_10.11_spmd, body=%wide.region_8.10_spmd.sunk | while | flops 543160320 | bytes 1362525 | solution.py:40
  241.9 2.3 multiply_reduce_fusion.20
  244.3 2.3 multiply_reduce_fusion.20
  246.8 2.3 multiply_reduce_fusion.20
  249.3 2.3 multiply_reduce_fusion.20
  251.7 9.8 %while.63 = (s32[]{:T(128)}, f32[4,2048]{1,0:T(4,128)S(1)}, f32[4,2048]{1,0:T(4,128)S(1)}, f32[512]{0:T(512)S(1)}, bf16[4,2048,256]{2,1,0:T(8,128)(2,1)}, /*inde...) while((s32[]{:T(128)}, f32[4,2048]{1,0:T(4,128)S(1)}, f32[4,2048]{1,0:T(4,128)S(1)}, f32[512]{0:T(512)S(1)}, ...), condition=%wide.region_18.19_spmd, body=%wide.region_16.18_spmd.sunk | while | flops 543160320 | bytes 1362525 | solution.py:40
  251.8 2.3 multiply_reduce_fusion.22
  254.2 2.3 multiply_reduce_fusion.22
  256.7 2.3 multiply_reduce_fusion.22
  259.1 2.3 multiply_reduce_fusion.22
  261.6 9.8 %while.65 = (s32[]{:T(128)}, f32[4,2048]{1,0:T(4,128)S(1)}, f32[4,2048]{1,0:T(4,128)S(1)}, f32[512]{0:T(512)S(1)}, bf16[4,2048,256]{2,1,0:T(8,128)(2,1)}, /*inde...) while((s32[]{:T(128)}, f32[4,2048]{1,0:T(4,128)S(1)}, f32[4,2048]{1,0:T(4,128)S(1)}, f32[512]{0:T(512)S(1)}, ...), condition=%wide.region_26.27_spmd, body=%wide.region_24.26_spmd.sunk | while | flops 543160320 | bytes 1362525 | solution.py:40
  261.6 2.3 multiply_reduce_fusion.24
  264.1 2.3 multiply_reduce_fusion.24
  266.6 2.3 multiply_reduce_fusion.24
  269.0 2.3 multiply_reduce_fusion.24
  271.5 1.2 fusion.18
  272.7 0.7 minimum_reduce_fusion
  273.4 16.9 %all-reduce = (f32[]{:T(128)}, f32[]{:T(128)}, f32[]{:T(128)}, f32[]{:T(128)}, f32[]{:T(128)}, /*index=5*/f32[]{:T(128)}) all-reduce(f32[]{:T(128)} %get-tuple-element.300, f32[]{:T(128)} %get-tuple-element.302, f32[]{:T(128)} %get-tuple-element.303, f32[]{:T(128)} %get-tuple-element.207, ...), channel_id=1, replica_groups=mesh['grp'=4,'dev'=8] {'dev'}, use_global_device_ids=true, to_apply=%region_28.29 | all-reduce | flops 6 | bytes 48 | tf_op jit(solution)/shard_map/psum | solution.py:46
  294.1 0.6 stack.27
  (66 shorter events, 3.1 us)
Async XLA Ops:
  7.2 135.3 %all-gather.2.cloned.1.call-start = ((), (), s32[]{:S(2)}) async-start(), calls=%async_computation | async-start | bytes 14155776 | tf_op jit(solution)/shard_map/all_gather | solution.py:23
  22.9 186.8 %all-reduce.3.cloned.1.call-start = ((), (), s32[]{:S(2)}) async-start(), calls=%async_computation.1 | async-start | bytes 3145728 | tf_op jit(solution)/shard_map/psum | solution.py:24
  209.8 1.9 copy-start
  261.6 9.9 %copy-start.1 = (f32[8192]{0:T(1024)S(1)}, f32[8192]{0:T(1024)}, u32[]{:S(2)}) copy-start(f32[8192]{0:T(1024)} %param.16) | copy-start | bytes 98308
Sparse Core Ops, SparseCore 0:
  23.0 119.4 all-gather.1
  150.8 58.9 all-reduce.2
